TPU v7x, 32 devices: a whole 2x2x4 slice. The times are simulated.
32 devices in a mesh: tm: 8 (over z, y), coef: 4 (over x, core).
Axes of the slice: x: 2, y: 2, z: 4, core: 2. Of those that a mesh axis runs over, the one named last changes fastest.
Arguments:
- design: bfloat16 [2048, 50176], P('tm', 'coef'), may hold values from -0.0390625 to 0.0390625
- observed: float32 [2048, 128], P('tm'), may hold values from -6 to 6
- slab_counts: int32 [8], P('tm'), may hold values from 128 to 256, as said below
- gap_mask: int32 [2048], P('tm'), may hold values 0 or 1
- filter_taps: float32 [128], replicated, may hold values from -0.5 to 1.2, as said below
- kaula_diag: float32 [50176], P('coef'), may hold values from 0.1 to 1
- precond: float32 [50176], P('coef'), may hold values from 0.3 to 3
Outputs:
- solution: float32 [50176, 128], P(('coef', 'tm'))
- residual: float32 [50176, 128], P(('coef', 'tm'))
Inputs may be any that keep to these rules, and one draw needn't show every extreme that they name: `slab_counts`: every slab holds at most 256 valid epochs, and some slab holds exactly 256. filter_taps[0] lies between 1 and 1.2.
All inputs are finite; a program needn't handle non-finite values. No bound on the sum of `gap_mask` on one device may be relied on, other than what follows from the above.
Results may differ from a plain program's by a relative error of at most 0.0065.
The roundings to bfloat16 on the way count: a program that leaves them out, or rounds other values in their place, can miss the bound.
Values may be sent and summed in bfloat16 or wider, within the bound.
No kernel may reach another device: no remote copies, remote signals or barrier semaphores. Data moves between devices by JAX's collectives and lax.ppermute only.
A program may use at most 64 MiB of HBM per device.

v0:
```python
import jax
import jax.numpy as jnp
from jax import lax
from jax.sharding import PartitionSpec as P

ITERS = 2


def shifted(value, axis, steps):
    count = lax.axis_size(axis)
    first, last = (max(0, -steps), min(count, count - steps))
    return lax.ppermute(value, axis, [(source, source + steps) for source in range(first, last)])


def toeplitz(pattern, band_len):
    tiled = jnp.tile(pattern, band_len)[: band_len * (2 * band_len - 1)]
    return tiled.reshape(band_len, 2 * band_len - 1)[:, :band_len]


def block_pair(filter_taps):
    band_len = filter_taps.shape[0]
    spacer = jnp.zeros((band_len,), jnp.float32)
    reversed_taps = filter_taps[:0:-1]
    lower = jnp.concatenate([filter_taps[:1], spacer, reversed_taps])
    upper = jnp.concatenate([jnp.zeros((1,), jnp.float32), reversed_taps, spacer])
    return (toeplitz(lower, band_len), toeplitz(upper, band_len))


def forward(values, lower_block, upper_block):
    band_len = lower_block.shape[0]
    blocks = values.reshape(-1, band_len, values.shape[1])
    tail_block = shifted(blocks[-1], "tm", 1)
    previous = jnp.concatenate([tail_block[None], blocks[:-1]], 0)
    result = jnp.einsum("ij,bjr->bir", lower_block, blocks, precision=lax.Precision.HIGHEST)
    result = result + jnp.einsum(
        "ij,bjr->bir", upper_block, previous, precision=lax.Precision.HIGHEST
    )
    return result.reshape(values.shape)


def backward(values, lower_block, upper_block):
    band_len = lower_block.shape[0]
    blocks = values.reshape(-1, band_len, values.shape[1])
    head_block = shifted(blocks[0], "tm", -1)
    following = jnp.concatenate([blocks[1:], head_block[None]], 0)
    result = jnp.einsum("ji,bjr->bir", lower_block, blocks, precision=lax.Precision.HIGHEST)
    result = result + jnp.einsum(
        "ji,bjr->bir", upper_block, following, precision=lax.Precision.HIGHEST
    )
    return result.reshape(values.shape)


def shards(design, observed, slab_counts, gap_mask, filter_taps, kaula_diag, precond):
    epoch_rows, coef_rows = design.shape
    owned_rows = coef_rows // lax.axis_size("tm")
    owner_index = lax.axis_index("tm")
    lower_block, upper_block = block_pair(filter_taps)
    position = jnp.arange(epoch_rows, dtype=jnp.int32)
    weight = ((gap_mask == 1) & (position < slab_counts[0])).astype(jnp.float32)[:, None]

    def weighted(values):
        inner = forward(weight * values, lower_block, upper_block)
        return (weight * backward(inner, lower_block, upper_block)).astype(jnp.bfloat16)

    def transposed_term(filtered):
        return lax.dot_general(
            design, filtered, (((0,), (0,)), ((), ())), preferred_element_type=jnp.float32
        )

    def collect_rows(filtered):
        return lax.psum_scatter(transposed_term(filtered), "tm", scatter_dimension=0, tiled=True)

    def global_sum(terms):
        return lax.psum(terms, ("tm", "coef"))

    kaula_col = lax.dynamic_slice_in_dim(kaula_diag, owner_index * owned_rows, owned_rows, 0)[
        :, None
    ]
    precond_col = lax.dynamic_slice_in_dim(precond, owner_index * owned_rows, owned_rows, 0)[
        :, None
    ]
    residual = collect_rows(weighted(observed))
    solution = jnp.zeros_like(residual)
    scaled = precond_col * residual
    direction = scaled
    norm_now = global_sum(jnp.sum(residual * scaled, 0))
    for iteration in range(ITERS):
        slab_values = lax.psum(
            jnp.dot(
                design,
                lax.all_gather(direction.astype(jnp.bfloat16), "tm", axis=0, tiled=True),
                preferred_element_type=jnp.float32,
            ),
            "coef",
        )
        image = collect_rows(weighted(slab_values)) + kaula_col * direction
        curvature = global_sum(jnp.sum(direction * image, 0))
        step_len = norm_now / curvature
        solution = solution + step_len * direction
        residual = residual - step_len * image
        if iteration + 1 < ITERS:
            scaled = precond_col * residual
            norm_next = global_sum(jnp.sum(residual * scaled, 0))
            direction = scaled + norm_next / norm_now * direction
            norm_now = norm_next
    return (solution, residual)


def solution(mesh):
    placed = (P("tm", "coef"), P("tm", None), P("tm"), P("tm"), P(), P("coef"), P("coef"))
    return jax.shard_map(
        shards,
        mesh=mesh,
        in_specs=placed,
        out_specs=(P(("coef", "tm"), None), P(("coef", "tm"), None)),
        check_vma=False,
    )
```

profile of v0, /device:TPU:0, one launch (start us, length us, event | category | flops | bytes accessed | tf_op | source)
XLA Modules:
  0.0 791.0 jit_solution(16113411345253262551)
XLA Ops:
  7.9 1.0 copy.30
  8.9 0.7 and_convert_fusion
  9.6 4.9 collective-permute-start
  14.5 0.7 slice.67
  15.3 0.7 pad_maximum_fusion.1
  17.5 1.3 collective-permute-start.1
  19.1 4.5 collective-permute-done.1
  24.1 6.5 convolution_bitcast_fusion.2
  30.6 8.0 %copy.74 = f32[12544,128]{1,0:T(8,128)} copy(f32[12544,128]{0,1:T(8,128)} %convolution_bitcast_fusion.2) | data formatting | bytes 12845056
  38.7 0.8 dynamic_slice.6
  39.4 120.5 %reduce-scatter.10.cloned.1.call-done = f32[1568,128]{1,0:T(8,128)} async-done(((f32[12544,128]{1,0:T(8,128)}), f32[1568,128]{1,0:T(8,128)}) %reduce-scatter.10.cloned.1.call-update) | async-done | bytes 802832
  159.9 1.4 copy.75
  161.4 0.9 copy.37
  162.4 60.2 %all-gather.3.cloned.1.call-done = bf16[12544,128]{1,0:T(8,128)(2,1)} async-done(((bf16[1568,128]{1,0:T(8,128)(2,1)}), bf16[12544,128]{1,0:T(8,128)(2,1)}) %all-gather.3.cloned.1.call-update) | async-done | bytes 3211280 | tf_op jit(solution)/shard_map/all_gather | solution.py:91
  222.6 6.7 convolution_bitcast_fusion.4
  229.3 30.5 %all-reduce.4.cloned.1.call-done = f32[256,128]{0,1:T(8,128)} async-done(((f32[256,128]{0,1:T(8,128)}), f32[256,128]{0,1:T(8,128)}) %all-reduce.4.cloned.1.call-update) | async-done | bytes 131088 | tf_op jit(solution)/shard_map/psum | solution.py:88
  259.9 0.9 broadcast_multiply_fusion.1
  260.8 3.4 collective-permute-start.2
  264.2 1.2 fusion.11
  265.4 0.7 collective-permute-done.2
  266.4 1.3 collective-permute-start.3
  268.0 4.9 collective-permute-done.3
  273.3 6.5 convolution_bitcast_fusion.1
  279.8 8.0 %copy.76 = f32[12544,128]{1,0:T(8,128)} copy(f32[12544,128]{0,1:T(8,128)} %convolution_bitcast_fusion.1) | data formatting | bytes 12845056
  287.9 0.8 dynamic_slice.7
  288.7 119.7 %reduce-scatter.12.cloned.1.call-done = f32[1568,128]{1,0:T(8,128)} async-done(((f32[12544,128]{1,0:T(8,128)}), f32[1568,128]{1,0:T(8,128)}) %reduce-scatter.12.cloned.1.call-update) | async-done | bytes 802832
  408.4 1.4 copy.77
  410.2 39.5 %all-reduce = (f32[128]{0:T(128)S(1)}, f32[128]{0:T(128)S(1)}) all-reduce(f32[128]{0:T(128)S(1)} %get-tuple-element.7, f32[128]{0:T(128)S(1)} %get-tuple-element.6), channel_id=1, replica_groups=mesh['tm'=8,'coef'=4] {'tm','coef'}, use_global_device_ids=true, to_apply=%region_2.0 | all-reduce | flops 256 | bytes 2048 | tf_op jit(solution)/shard_map/psum | solution.py:74
  450.0 39.6 %psum.45 = f32[128]{0:T(128)S(1)} all-reduce(f32[128]{0:T(128)S(1)} %fusion.7), channel_id=1, replica_groups=mesh['tm'=8,'coef'=4] {'tm','coef'}, use_global_device_ids=true, to_apply=%region_8.0 | all-reduce | flops 128 | bytes 1024 | tf_op jit(solution)/shard_map/psum | solution.py:74
  490.0 0.9 copy.44
  491.2 60.7 %all-gather.5.cloned.1.call-done = bf16[12544,128]{1,0:T(8,128)(2,1)} async-done(((bf16[1568,128]{1,0:T(8,128)(2,1)}), bf16[12544,128]{1,0:T(8,128)(2,1)}) %all-gather.5.cloned.1.call-update) | async-done | bytes 3211280 | tf_op jit(solution)/shard_map/all_gather | solution.py:91
  551.9 6.7 convolution_bitcast_fusion.3
  558.6 30.6 %all-reduce.6.cloned.1.call-done = f32[256,128]{0,1:T(8,128)} async-done(((f32[256,128]{0,1:T(8,128)}), f32[256,128]{0,1:T(8,128)}) %all-reduce.6.cloned.1.call-update) | async-done | bytes 131088 | tf_op jit(solution)/shard_map/psum | solution.py:88
  589.2 0.9 broadcast_multiply_fusion
  590.1 3.4 collective-permute-start.4
  593.5 1.2 fusion.8
  594.7 0.7 collective-permute-done.4
  595.7 1.3 collective-permute-start.5
  597.3 4.9 collective-permute-done.5
  602.6 6.5 convolution_bitcast_fusion
  609.2 8.0 %copy.78 = f32[12544,128]{1,0:T(8,128)} copy(f32[12544,128]{0,1:T(8,128)} %convolution_bitcast_fusion) | data formatting | bytes 12845056
  617.2 120.6 %reduce-scatter.14.cloned.1.call-done = f32[1568,128]{1,0:T(8,128)} async-done(((f32[12544,128]{1,0:T(8,128)}), f32[1568,128]{1,0:T(8,128)}) %reduce-scatter.14.cloned.1.call-update) | async-done | bytes 802832
  737.8 1.4 copy.79
  739.2 0.5 multiply_reduce_fusion
  739.7 39.5 %psum.47 = f32[128]{0:T(128)S(1)} all-reduce(f32[128]{0:T(128)S(1)} %multiply_reduce_fusion), channel_id=1, replica_groups=mesh['tm'=8,'coef'=4] {'tm','coef'}, use_global_device_ids=true, to_apply=%region_12.0 | all-reduce | flops 128 | bytes 1024 | tf_op jit(solution)/shard_map/psum | solution.py:74
  779.2 1.5 multiply_subtract_fusion
  780.7 2.3 copy.52
  783.0 1.2 copy.51
  (49 shorter events, 5.9 us)
Async XLA Ops:
  7.2 152.8 %reduce-scatter.10.cloned.1.call-start = ((), (), s32[]{:S(2)}) async-start(), calls=%async_computation.7 | async-start | bytes 7225344
  9.6 7.6 collective-permute-start
  17.5 6.2 collective-permute-start.1
  38.6 184.0 %all-gather.3.cloned.1.call-start = ((), (), s32[]{:S(2)}) async-start(), calls=%async_computation.3 | async-start | bytes 3612672 | tf_op jit(solution)/shard_map/all_gather | solution.py:91
  162.4 97.5 %all-reduce.4.cloned.1.call-start = ((), (), s32[]{:S(2)}) async-start(), calls=%async_computation.4 | async-start | bytes 262144 | tf_op jit(solution)/shard_map/psum | solution.py:88
  229.3 179.1 %reduce-scatter.12.cloned.1.call-start = ((), (), s32[]{:S(2)}) async-start(), calls=%async_computation.8 | async-start | bytes 7225344
  260.8 5.3 collective-permute-start.2
  266.4 6.5 collective-permute-start.3
  287.8 264.0 %all-gather.5.cloned.1.call-start = ((), (), s32[]{:S(2)}) async-start(), calls=%async_computation.5 | async-start | bytes 3612672 | tf_op jit(solution)/shard_map/all_gather | solution.py:91
  490.9 98.3 %all-reduce.6.cloned.1.call-start = ((), (), s32[]{:S(2)}) async-start(), calls=%async_computation.6 | async-start | bytes 262144 | tf_op jit(solution)/shard_map/psum | solution.py:88
  558.6 179.2 %reduce-scatter.14.cloned.1.call-start = ((), (), s32[]{:S(2)}) async-start(), calls=%async_computation.9 | async-start | bytes 7225344
  590.1 5.3 collective-permute-start.4
  595.7 6.5 collective-permute-start.5
Sparse Core Ops, SparseCore 0:
  38.7 121.1 reduce-scatter.9
  162.7 59.8 all-gather.2
  229.4 30.4 all-reduce.3
  288.0 120.4 reduce-scatter.11
  491.1 60.7 all-gather.4
  558.7 30.4 all-reduce.5
  617.3 120.4 reduce-scatter.13
where the time goes:
time: 792 us; the launch traced here: 791 us
  waiting for transfers between devices  559 us (71%)
  blocking collectives  119 us (15%)
  matrix products  38.3 us (5%)
  local copies, waits for them, and re-layouts  38.1 us (5%)
  starting transfers between devices  16 us (2%)
  between operations  15.1 us (2%)
    unnamed x10, waiting for transfers between devices  361 us
    all_gather x2, waiting for transfers between devices, shards(): lax.all_gather(direction.astype(jnp.bfloat16), 'tm', axis=0, tiled=True)  121 us
    psum x3, blocking collectives, global_sum(): return lax.psum(terms, ('tm', 'coef'))  119 us
    psum x2, waiting for transfers between devices, shards(): lax.psum(jnp.dot(design, lax.all_gather(direction.astype(jnp.bfloat16), '...  61.1 us
    unnamed x12, local copies, waits for them, and re-layouts  32.9 us
    dot_general x3, matrix products, transposed_term(): lax.dot_general(design, filtered, (((0,), (0,)), ((), ())), preferred_ele...  19.6 us
  transfers between devices with their start and end apart: 13, of which 12 were waited for; matrix products, arithmetic and copies ran while one was open for 1% of the time, Pallas kernels for 0%

commit v1 on v0

v1 whole, which is shorter than its diff:
```python
import jax
import jax.numpy as jnp
from jax import lax
from jax.sharding import PartitionSpec as P

ITERS = 2
LANES = 128
BOTH = ("tm", "coef")


def toeplitz(pattern, band_len):
    tiled = jnp.tile(pattern, band_len)[: band_len * (2 * band_len - 1)]
    return tiled.reshape(band_len, 2 * band_len - 1)[:, :band_len]


def block_pair(filter_taps):
    band_len = filter_taps.shape[0]
    spacer = jnp.zeros((band_len,), jnp.float32)
    reversed_taps = filter_taps[:0:-1]
    lower = jnp.concatenate([filter_taps[:1], spacer, reversed_taps])
    upper = jnp.concatenate([jnp.zeros((1,), jnp.float32), reversed_taps, spacer])
    return (toeplitz(lower, band_len), toeplitz(upper, band_len))


def forward(values, lower_block, upper_block):
    band_len = lower_block.shape[0]
    blocks = values.reshape(-1, band_len, values.shape[1])
    previous = jnp.concatenate([jnp.zeros_like(blocks[:1]), blocks[:-1]], 0)
    result = jnp.einsum("ij,bjr->bir", lower_block, blocks, precision=lax.Precision.HIGHEST)
    result = result + jnp.einsum(
        "ij,bjr->bir", upper_block, previous, precision=lax.Precision.HIGHEST
    )
    return result.reshape(values.shape)


def backward(values, lower_block, upper_block):
    band_len = lower_block.shape[0]
    blocks = values.reshape(-1, band_len, values.shape[1])
    following = jnp.concatenate([blocks[1:], jnp.zeros_like(blocks[:1])], 0)
    result = jnp.einsum("ji,bjr->bir", lower_block, blocks, precision=lax.Precision.HIGHEST)
    result = result + jnp.einsum(
        "ji,bjr->bir", upper_block, following, precision=lax.Precision.HIGHEST
    )
    return result.reshape(values.shape)


def shards(design, observed, slab_counts, gap_mask, filter_taps, kaula_diag, precond):
    epoch_rows, coef_rows = design.shape
    slabs = lax.axis_size("tm")
    owned_rows = coef_rows // slabs
    owner_index = lax.axis_index("tm")

    tile = LANES if coef_rows % LANES == 0 else owned_rows
    tiles = coef_rows // tile
    width = max(
        -(-(slab + 1) * owned_rows // tile) - slab * owned_rows // tile for slab in range(slabs)
    )
    first_tiles = [min(slab * owned_rows // tile, tiles - width) for slab in range(slabs)]
    window = width * tile
    begins = [first * tile for first in first_tiles]
    begin = jnp.array(begins, jnp.int32)[owner_index]
    offset = owner_index * owned_rows - begin

    pieces = jnp.stack([design[:, start : start + window] for start in begins])
    columns = lax.all_to_all(pieces, "tm", 0, 0).reshape(slabs * epoch_rows, window)

    position = jnp.arange(epoch_rows, dtype=jnp.int32)
    own_weight = ((gap_mask == 1) & (position < slab_counts[0])).astype(jnp.float32)
    packed = jnp.concatenate(
        [observed, jnp.broadcast_to(own_weight[:, None], (epoch_rows, LANES))], 1
    )
    packed = lax.all_gather(packed, "tm", axis=0, tiled=True)
    observed_all = packed[:, : observed.shape[1]]
    weight = packed[:, observed.shape[1] : observed.shape[1] + 1]
    lower_block, upper_block = block_pair(filter_taps)

    def weighted(values):
        inner = forward(weight * values, lower_block, upper_block)
        return (weight * backward(inner, lower_block, upper_block)).astype(jnp.bfloat16)

    def transposed(filtered):
        return lax.dot_general(
            columns, filtered, (((0,), (0,)), ((), ())), preferred_element_type=jnp.float32
        )

    def reduced(vector, rows):
        product = jnp.dot(
            columns, vector.astype(jnp.bfloat16), preferred_element_type=jnp.float32
        )
        extra = jnp.stack(rows + [jnp.zeros_like(rows[0])] * (8 - len(rows)))
        total = lax.psum(jnp.concatenate([product, extra]), BOTH)
        return total[: product.shape[0]], [total[product.shape[0] + i] for i in range(len(rows))]

    local = jnp.arange(window, dtype=jnp.int32)
    owned = (local >= offset) & (local < offset + owned_rows)

    def window_of(values):
        cut = lax.dynamic_slice_in_dim(values, begin, window, 0)
        return jnp.where(owned, cut, 0.0)[:, None]

    kaula_col = window_of(kaula_diag)
    precond_col = window_of(precond)

    residual = transposed(weighted(observed_all))
    solution = jnp.zeros_like(residual)
    direction = None
    for iteration in range(ITERS):
        scaled = precond_col * residual
        rows = [jnp.sum(residual * scaled, 0), jnp.sum(kaula_col * scaled * scaled, 0)]
        if iteration:
            rows.append(jnp.sum(kaula_col * scaled * direction, 0))
        product, sums = reduced(scaled, rows)
        if iteration:
            ratio = sums[0] / norm_now
            direction = scaled + ratio * direction
            slab_values = product + ratio * slab_values
            ridge = sums[1] + 2.0 * ratio * sums[2] + ratio * ratio * ridge
        else:
            direction, slab_values, ridge = scaled, product, sums[1]
        norm_now = sums[0]
        filtered = weighted(slab_values)
        curvature = jnp.sum(slab_values * filtered.astype(jnp.float32), 0) + ridge
        image = transposed(filtered) + kaula_col * direction
        step_len = norm_now / curvature
        solution = solution + step_len * direction
        residual = residual - step_len * image
    return tuple(
        lax.dynamic_slice_in_dim(values, offset, owned_rows, 0) for values in (solution, residual)
    )


def solution(mesh):
    placed = (P("tm", "coef"), P("tm", None), P("tm"), P("tm"), P(), P("coef"), P("coef"))
    return jax.shard_map(
        shards,
        mesh=mesh,
        in_specs=placed,
        out_specs=(P(("coef", "tm"), None), P(("coef", "tm"), None)),
        check_vma=False,
    )
```

time: 792 us -> 520 us (0.66)
  waiting for transfers between devices: 559 us -> 418 us
  blocking collectives: 119 us -> 0 us
  local copies, waits for them, and re-layouts: 38.1 us -> 21.2 us
  starting transfers between devices: 16 us -> 7.75 us
    unnamed x10 -> x3, waiting for transfers between devices: 361 us -> 0.05 us
    psum x2, waiting for transfers between devices: 61.1 us -> 260 us  [reduced(): total = lax.psum(jnp.concatenate([product, extra]), BOTH)]
    psum x3 -> x0, blocking collectives: 119 us -> none  [global_sum(): return lax.psum(terms, ('tm', 'coef'))]
    unnamed x12 -> x26, local copies, waits for them, and re-layouts: 32.9 us -> 12 us
    all_gather x2 -> x1, waiting for transfers between devices: 121 us -> 140 us  [shards(): packed = lax.all_gather(packed, 'tm', axis=0, tiled=True)]
    all_to_all x0 -> x1, waiting for transfers between devices: none -> 17.8 us  [shards(): lax.all_to_all(pieces, 'tm', 0, 0).reshape(slabs * epoch_rows, window)]
    ppermute x6 -> x0, waiting for transfers between devices: 15.7 us -> none  [shifted(): lax.ppermute(value, axis, [(source, source + steps) for source in range(f...]
    ppermute x6 -> x0, starting transfers between devices: 15.5 us -> none  [shifted(): lax.ppermute(value, axis, [(source, source + steps) for source in range(f...]
  transfers between devices with their start and end apart: 13 -> 4, of which waited for: 12 -> 4; matrix products, arithmetic and copies ran while one was open for 1% -> 3% of each run, Pallas kernels for 0% -> 0%
where the time goes in v1:
time: 520 us; the launch traced here: 519 us
  waiting for transfers between devices  418 us (80%)
  matrix products  43.2 us (8%)
  local copies, waits for them, and re-layouts  21.2 us (4%)
  between operations  17.4 us (3%)
  other arithmetic  11.4 us (2%)
  starting transfers between devices  7.75 us (1%)
    psum x2, waiting for transfers between devices, reduced(): total = lax.psum(jnp.concatenate([product, extra]), BOTH)  260 us
    all_gather x1, waiting for transfers between devices, shards(): packed = lax.all_gather(packed, 'tm', axis=0, tiled=True)  140 us
    all_to_all x1, waiting for transfers between devices, shards(): lax.all_to_all(pieces, 'tm', 0, 0).reshape(slabs * epoch_rows, window)  17.8 us
    dot_general x3, matrix products, transposed(): lax.dot_general(columns, filtered, (((0,), (0,)), ((), ())), preferred_el...  15.7 us
    unnamed x26, local copies, waits for them, and re-layouts  12 us
  transfers between devices with their start and end apart: 4, of which 4 were waited for; matrix products, arithmetic and copies ran while one was open for 3% of the time, Pallas kernels for 0%

profile of v1, /device:TPU:0, one launch (start us, length us, event | category | flops | bytes accessed | tf_op | source)
XLA Modules:
  0.0 519.3 jit_solution(8027475732928325640)
XLA Ops:
  7.2 2.3 bitcast_dynamic-update-slice_fusion.7
  9.5 2.3 bitcast_dynamic-update-slice_fusion.6
  11.7 2.2 bitcast_dynamic-update-slice_fusion.5
  13.9 2.1 bitcast_dynamic-update-slice_fusion.4
  16.1 1.0 bitcast_dynamic-update-slice_fusion.3
  17.0 1.0 bitcast_dynamic-update-slice_fusion.2
  18.0 1.0 bitcast_dynamic-update-slice_fusion.1
  19.0 1.0 bitcast_dynamic-update-slice_fusion
  20.1 7.5 %all-to-all-start = ((bf16[8,256,1664]{2,1,0:T(8,128)(2,1)}), bf16[8,256,1664]{2,1,0:T(8,128)(2,1)}, u32[]{:S(2)}, u32[]{:S(2)}) async-start(bf16[8,256,1664]{2,1,0:T(8,128)(2,1)} %bitcast_dynamic-update-slice_fusion), calls=%async_computation | async-start | bytes 13631488 | tf_op jit(solution)/shard_map/all_to_all | solution.py:65
  28.3 0.7 pad_maximum_fusion
  29.1 0.6 dynamic_slice.15
  32.1 0.3 reshape.59
  32.5 0.3 reshape.60
  33.5 0.8 dynamic-slice_select_fusion
  34.3 0.8 dynamic-slice_select_fusion.1
  35.1 140.5 %all-gather.2.cloned.1.call-done = f32[2048,256]{1,0:T(8,128)} async-done(((f32[256,256]{1,0:T(8,128)}), f32[2048,256]{1,0:T(8,128)}) %all-gather.2.cloned.1.call-update) | async-done | bytes 2097168 | tf_op jit(solution)/shard_map/all_gather | solution.py:72
  175.5 1.6 slice_reduce_fusion
  177.1 1.6 slice_multiply_fusion
  178.8 1.8 fusion.29
  180.6 1.7 fusion.4
  182.3 1.1 fusion.26
  183.4 1.1 fusion.6
  184.5 17.8 %all-to-all-done = bf16[8,256,1664]{2,1,0:T(8,128)(2,1)} async-done(((bf16[8,256,1664]{2,1,0:T(8,128)(2,1)}), bf16[8,256,1664]{2,1,0:T(8,128)(2,1)}, u32[]{:S(2)}, u32[]{:S(2)}) %all-to-all-start) | async-done | bytes 6815776 | tf_op jit(solution)/shard_map/all_to_all | solution.py:65
  202.3 5.3 %fusion.15 = (f32[128]{0:T(128)S(1)}, f32[128]{0:T(128)S(1)}, f32[1664,128]{1,0:T(8,128)S(1)}) fusion(f32[1664]{0:T(1024)S(1)} %dynamic-slice_select_fusion, f32[1664]{0:T(1024)S(1)} %dynamic-slice_select_fusion.1, bf16[2048,1664]{1,0:T(8,128)(2,1)} %bitcast.8, bf16[2048,128]{1,0:T(8,128)(2,1)S(1)} %bitcast.152), kind=kOutput, calls=%fused_computation.38 | convolution fusion | flops 873692928 | bytes 8206336 | tf_op jit(solution)/shard_map/dot_general | solution.py:82
  207.6 5.3 %fusion.20 = f32[2048,128]{1,0:T(8,128)S(1)} fusion(bf16[2048,1664]{1,0:T(8,128)(2,1)} %bitcast.8, f32[1664,128]{1,0:T(8,128)S(1)} %get-tuple-element.13, f32[1664]{0:T(1024)S(1)} %dynamic-slice_select_fusion.1), kind=kOutput, calls=%fused_computation.57 | convolution fusion | flops 872841216 | bytes 8722944 | tf_op jit(solution)/shard_map/dot_general | solution.py:87
  212.9 2.3 concatenate.42
  215.2 0.2 all-reduce.11.cloned.1.call-start
  215.4 129.3 %all-reduce.9.cloned.1.call-done = f32[2056,128]{1,0:T(8,128)} async-done(((f32[2056,128]{1,0:T(8,128)}), f32[2056,128]{1,0:T(8,128)}) %all-reduce.9.cloned.1.call-update) | async-done | bytes 1052688 | tf_op jit(solution)/shard_map/psum | solution.py:91
  344.7 1.6 slice_multiply_fusion.1
  346.4 1.8 fusion.28
  348.2 1.7 fusion.3
  349.9 1.1 fusion.25
  351.0 1.2 fusion.10
  352.2 0.4 multiply_reduce_fusion.1
  352.5 5.4 %fusion.17 = (f32[128]{0:T(128)S(1)}, f32[128]{0:T(128)S(1)}, f32[128]{0:T(128)S(1)}, f32[1664,128]{1,0:T(8,128)S(1)}) fusion(f32[1664,128]{1,0:T(8,128)S(1)} %get-tuple-element.13, f32[1664]{0:T(1024)S(1)} %dynamic-slice_select_fusion, f32[1664]{0:T(1024)S(1)} %dynamic-slice_select_fusion.1, bf16[2048,1664]{1,0:T(8,128)(2,1)} %bitcast.8, ...), kind=kOutput, calls=%fused_computation.40 | convolution fusion | flops 875183744 | bytes 9059328 | tf_op jit(solution)/shard_map/dot_general | solution.py:82
  358.0 5.1 fusion.21
  363.0 2.5 concatenate.45
  365.6 130.8 %all-reduce.11.cloned.1.call-done = f32[2056,128]{1,0:T(8,128)} async-done(((f32[2056,128]{1,0:T(8,128)}), f32[2056,128]{1,0:T(8,128)}) %all-reduce.11.cloned.1.call-update) | async-done | bytes 1052688 | tf_op jit(solution)/shard_map/psum | solution.py:91
  496.4 0.7 slice_divide_fusion
  497.1 1.4 multiply_add_fusion
  498.6 1.6 broadcast_multiply_fusion
  500.2 1.8 fusion.27
  502.0 1.7 fusion.2
  503.7 1.1 fusion.24
  504.8 1.2 fusion.9
  506.0 4.9 fusion.37
  511.0 0.4 multiply_reduce_fusion
  511.3 1.5 dynamic-slice_subtract_fusion
  (39 shorter events, 1.0 us)
Async XLA Ops:
  7.2 8.9 %copy-start.1 = (bf16[256,12544]{1,0:T(8,128)(2,1)S(1)}, bf16[256,12544]{1,0:T(8,128)(2,1)}, u32[]{:S(2)}) copy-start(bf16[256,12544]{1,0:T(8,128)(2,1)} %param.8) | copy-start | bytes 19267588
  20.0 8.2 %copy-start.5 = (s32[256]{0:T(256)S(1)}, s32[256]{0:T(256)}, u32[]{:S(2)}) copy-start(s32[256]{0:T(256)} %param.11) | copy-start | bytes 3076
  20.0 8.3 %copy-start.4 = (f32[256,128]{1,0:T(8,128)S(1)}, f32[256,128]{1,0:T(8,128)}, u32[]{:S(2)}) copy-start(f32[256,128]{1,0:T(8,128)} %param.9) | copy-start | bytes 393220
  20.0 9.1 %copy-start.7 = (s32[8]{0:T(128)S(1)}, s32[8]{0:T(128)}, u32[]{:S(2)}) copy-start(s32[8]{0:T(128)} %constant.9.clone) | copy-start | bytes 100
  20.1 11.6 %copy-start.6 = (f32[128]{0:T(128)S(1)}, f32[128]{0:T(128)}, u32[]{:S(2)}) copy-start(f32[128]{0:T(128)} %param.12) | copy-start | bytes 1540
  20.1 182.2 %all-to-all-start = ((bf16[8,256,1664]{2,1,0:T(8,128)(2,1)}), bf16[8,256,1664]{2,1,0:T(8,128)(2,1)}, u32[]{:S(2)}, u32[]{:S(2)}) async-start(bf16[8,256,1664]{2,1,0:T(8,128)(2,1)} %bitcast_dynamic-update-slice_fusion), calls=%async_computation | async-start | bytes 13631488 | tf_op jit(solution)/shard_map/all_to_all | solution.py:65
  27.5 148.0 %all-gather.2.cloned.1.call-start = ((), (), s32[]{:S(2)}) async-start(), calls=%async_computation.1 | async-start | bytes 2359296 | tf_op jit(solution)/shard_map/all_gather | solution.py:72
  29.1 315.7 %all-reduce.9.cloned.1.call-start = ((), (), s32[]{:S(2)}) async-start(), calls=%async_computation.2 | async-start | bytes 2105344 | tf_op jit(solution)/shard_map/psum | solution.py:91
  207.6 145.0 %copy-start.3 = (f32[1664,128]{1,0:T(8,128)}, f32[1664,128]{1,0:T(8,128)S(1)}, u32[]{:S(2)}) copy-start(f32[1664,128]{1,0:T(8,128)S(1)} %get-tuple-element.13) | copy-start | bytes 2555908
  215.2 281.2 %all-reduce.11.cloned.1.call-start = ((), (), s32[]{:S(2)}) async-start(), calls=%async_computation.3 | async-start | bytes 2105344 | tf_op jit(solution)/shard_map/psum | solution.py:91
  346.3 5.9 %copy-start = (f32[2056,128]{1,0:T(8,128)S(1)}, f32[2056,128]{1,0:T(8,128)}, u32[]{:S(2)}) copy-start(f32[2056,128]{1,0:T(8,128)} %all-reduce.9.cloned.1.call-done) | copy-start | bytes 3158020
  504.8 6.1 %copy-start.2 = (f32[2056,128]{1,0:T(8,128)S(1)}, f32[2056,128]{1,0:T(8,128)}, u32[]{:S(2)}) copy-start(f32[2056,128]{1,0:T(8,128)} %all-reduce.11.cloned.1.call-done) | copy-start | bytes 3158020
Sparse Core Ops, SparseCore 0:
  31.0 144.4 all-gather.1
  215.3 129.3 all-reduce.8
  365.7 130.7 all-reduce.10

commit v2 on v1

--- a/solution.py
+++ b/solution.py
@@ -5,7 +5,6 @@
 
 ITERS = 2
 LANES = 128
-BOTH = ("tm", "coef")
 
 
 def toeplitz(pattern, band_len):
@@ -44,6 +43,33 @@
     return result.reshape(values.shape)
 
 
+def exchanged(value, axis, distance):
+    return lax.ppermute(
+        value, axis, [(index, index ^ distance) for index in range(lax.axis_size(axis))]
+    )
+
+
+def total_sum(value):
+    parts = lax.axis_size("coef")
+    own = lax.axis_index("coef")
+    blocks = value.reshape(parts, -1, value.shape[1])
+
+    def block(distance):
+        return lax.dynamic_index_in_dim(blocks, own ^ distance, 0, keepdims=False)
+
+    received = [exchanged(block(distance), "coef", distance) for distance in range(1, parts)]
+    mine = sum(received, block(0))
+    distance = 1
+    while distance < lax.axis_size("tm"):
+        mine = mine + exchanged(mine, "tm", distance)
+        distance *= 2
+    gathered = [mine] + [exchanged(mine, "coef", distance) for distance in range(1, parts)]
+    result = jnp.zeros_like(blocks)
+    for distance, part in enumerate(gathered):
+        result = lax.dynamic_update_index_in_dim(result, part, own ^ distance, 0)
+    return result.reshape(value.shape)
+
+
 def shards(design, observed, slab_counts, gap_mask, filter_taps, kaula_diag, precond):
     epoch_rows, coef_rows = design.shape
     slabs = lax.axis_size("tm")
@@ -66,12 +92,12 @@
 
     position = jnp.arange(epoch_rows, dtype=jnp.int32)
     own_weight = ((gap_mask == 1) & (position < slab_counts[0])).astype(jnp.float32)
-    packed = jnp.concatenate(
-        [observed, jnp.broadcast_to(own_weight[:, None], (epoch_rows, LANES))], 1
-    )
-    packed = lax.all_gather(packed, "tm", axis=0, tiled=True)
-    observed_all = packed[:, : observed.shape[1]]
-    weight = packed[:, observed.shape[1] : observed.shape[1] + 1]
+    columns_count = observed.shape[1]
+    weight_rows = own_weight.reshape(-1, columns_count)
+    blank = jnp.zeros((-weight_rows.shape[0] % 8, columns_count), jnp.float32)
+    packed = lax.all_gather(jnp.concatenate([observed, weight_rows, blank]), "tm", axis=0)
+    observed_all = packed[:, :epoch_rows].reshape(-1, columns_count)
+    weight = packed[:, epoch_rows : epoch_rows + weight_rows.shape[0]].reshape(-1, 1)
     lower_block, upper_block = block_pair(filter_taps)
 
     def weighted(values):
@@ -87,8 +113,10 @@
         product = jnp.dot(
             columns, vector.astype(jnp.bfloat16), preferred_element_type=jnp.float32
         )
-        extra = jnp.stack(rows + [jnp.zeros_like(rows[0])] * (8 - len(rows)))
-        total = lax.psum(jnp.concatenate([product, extra]), BOTH)
+        unit = 8 * lax.axis_size("coef")
+        spare = -(product.shape[0] + len(rows)) % unit
+        extra = jnp.stack(rows + [jnp.zeros_like(rows[0])] * spare)
+        total = total_sum(jnp.concatenate([product, extra]))
         return total[: product.shape[0]], [total[product.shape[0] + i] for i in range(len(rows))]
 
     local = jnp.arange(window, dtype=jnp.int32)

time: 520 us -> 370 us (0.71)
  waiting for transfers between devices: 418 us -> 261 us
  starting transfers between devices: 7.75 us -> 16.5 us
    psum x2 -> x0, waiting for transfers between devices: 260 us -> none  [reduced(): total = lax.psum(jnp.concatenate([product, extra]), BOTH)]
    ppermute x0 -> x18, waiting for transfers between devices: none -> 104 us  [exchanged(): lax.ppermute(value, axis, [(index, index ^ distance) for index in range(l...]
    all_to_all x1, waiting for transfers between devices: 17.8 us -> 0.01 us  [shards(): lax.all_to_all(pieces, 'tm', 0, 0).reshape(slabs * epoch_rows, window)]
    all_gather x1, waiting for transfers between devices: 140 us -> 156 us  [shards(): lax.all_gather(jnp.concatenate([observed, weight_rows, blank]), 'tm', axi...]
    ppermute x0 -> x18, starting transfers between devices: none -> 8.98 us  [exchanged(): lax.ppermute(value, axis, [(index, index ^ distance) for index in range(l...]
    unnamed x26 -> x22, local copies, waits for them, and re-layouts: 12 us -> 12.1 us
  transfers between devices with their start and end apart: 4 -> 20, of which waited for: 4 -> 15; matrix products, arithmetic and copies ran while one was open for 3% -> 3% of each run, Pallas kernels for 0% -> 0%
where the time goes in v2:
time: 370 us; the launch traced here: 369 us
  waiting for transfers between devices  261 us (71%)
  matrix products  44.2 us (12%)
  local copies, waits for them, and re-layouts  21.6 us (6%)
  between operations  17.7 us (5%)
  starting transfers between devices  16.5 us (4%)
  other arithmetic  8.36 us (2%)
    all_gather x1, waiting for transfers between devices, shards(): lax.all_gather(jnp.concatenate([observed, weight_rows, blank]), 'tm', axi...  156 us
    ppermute x18, waiting for transfers between devices, exchanged(): lax.ppermute(value, axis, [(index, index ^ distance) for index in range(l...  104 us
    dot_general x3, matrix products, transposed(): lax.dot_general(columns, filtered, (((0,), (0,)), ((), ())), preferred_el...  15.4 us
    unnamed x22, local copies, waits for them, and re-layouts  12.1 us
    dot_general x2, matrix products, reduced(): jnp.dot(columns, vector.astype(jnp.bfloat16), preferred_element_type=jnp....  11.3 us
    ppermute x18, starting transfers between devices, exchanged(): lax.ppermute(value, axis, [(index, index ^ distance) for index in range(l...  8.98 us
    all_to_all x1, starting transfers between devices, shards(): lax.all_to_all(pieces, 'tm', 0, 0).reshape(slabs * epoch_rows, window)  7.45 us
  transfers between devices with their start and end apart: 20, of which 15 were waited for; matrix products, arithmetic and copies ran while one was open for 3% of the time, Pallas kernels for 0%

profile of v2, /device:TPU:0, one launch (start us, length us, event | category | flops | bytes accessed | tf_op | source)
XLA Modules:
  0.0 369.0 jit_solution(15584548592359763293)
XLA Ops:
  7.2 2.3 bitcast_dynamic-update-slice_fusion.7
  9.4 2.4 bitcast_dynamic-update-slice_fusion.6
  11.8 2.2 bitcast_dynamic-update-slice_fusion.5
  14.0 2.1 bitcast_dynamic-update-slice_fusion.4
  18.1 1.0 bitcast_dynamic-update-slice_fusion.1
  19.1 1.0 bitcast_dynamic-update-slice_fusion
  20.1 7.5 %all-to-all-start = ((bf16[8,256,1664]{2,1,0:T(8,128)(2,1)}), bf16[8,256,1664]{2,1,0:T(8,128)(2,1)}, u32[]{:S(2)}, u32[]{:S(2)}) async-start(bf16[8,256,1664]{2,1,0:T(8,128)(2,1)} %bitcast_dynamic-update-slice_fusion), calls=%async_computation | async-start | bytes 13631488 | tf_op jit(solution)/shard_map/all_to_all | solution.py:91
  34.3 156.3 %all-gather.3.cloned.1.call-done = f32[2112,128]{1,0:T(8,128)} async-done(((f32[264,128]{1,0:T(8,128)}), f32[2112,128]{1,0:T(8,128)}) %all-gather.3.cloned.1.call-update) | async-done | bytes 1081360 | tf_op jit(solution)/shard_map/all_gather | solution.py:98
  190.6 1.3 slice.129
  192.7 2.1 fusion.11
  195.1 1.7 fusion.4
  196.8 1.1 fusion.33
  197.9 1.1 fusion.6
  199.0 5.2 %fusion.17 = (f32[128]{0:T(128)S(1)}, f32[128]{0:T(128)S(1)}, f32[1664,128]{1,0:T(8,128)S(1)}) fusion(f32[1664]{0:T(1024)S(1)} %get-tuple-element.29, f32[1664]{0:T(1024)S(1)} %get-tuple-element.30, bf16[2048,1664]{1,0:T(8,128)(2,1)} %bitcast.8, bf16[2048,128]{1,0:T(8,128)(2,1)S(1)} %bitcast.224), kind=kOutput, calls=%fused_computation.39 | convolution fusion | flops 873692928 | bytes 8206336 | tf_op jit(solution)/shard_map/dot_general | solution.py:108
  204.3 5.3 %fusion.23 = f32[2048,128]{1,0:T(8,128)S(1)} fusion(bf16[2048,1664]{1,0:T(8,128)(2,1)} %bitcast.8, f32[1664,128]{1,0:T(8,128)S(1)} %get-tuple-element.23, f32[1664]{0:T(1024)S(1)} %get-tuple-element.30), kind=kOutput, calls=%fused_computation.59 | convolution fusion | flops 872841216 | bytes 8722944 | tf_op jit(solution)/shard_map/dot_general | solution.py:113
  210.8 1.5 collective-permute-start.1
  212.7 7.0 %collective-permute-done.2 = f32[520,128]{1,0:T(8,128)S(1)} collective-permute-done((f32[520,128]{1,0:T(8,128)}, f32[520,128]{1,0:T(8,128)S(1)}, u32[]{:S(2)}, u32[]{:S(2)}) %collective-permute-start.2) | collective-permute-done | bytes 266272 | tf_op jit(solution)/shard_map/ppermute | solution.py:47
  219.7 5.7 %collective-permute-done.1 = f32[520,128]{1,0:T(8,128)S(1)} collective-permute-done((f32[520,128]{1,0:T(8,128)S(1)}, f32[520,128]{1,0:T(8,128)S(1)}, u32[]{:S(2)}, u32[]{:S(2)}) %collective-permute-start.1) | collective-permute-done | bytes 266272 | tf_op jit(solution)/shard_map/ppermute | solution.py:47
  225.4 1.0 fusion.30
  226.6 8.4 %collective-permute-done.3 = f32[520,128]{1,0:T(8,128)S(1)} collective-permute-done((f32[520,128]{1,0:T(8,128)S(1)}, f32[520,128]{1,0:T(8,128)S(1)}, u32[]{:S(2)}, u32[]{:S(2)}) %collective-permute-start.3) | collective-permute-done | bytes 266272 | tf_op jit(solution)/shard_map/ppermute | solution.py:47
  235.0 7.5 %collective-permute-done.4 = f32[520,128]{1,0:T(8,128)S(1)} collective-permute-done((f32[520,128]{1,0:T(8,128)S(1)}, f32[520,128]{1,0:T(8,128)S(1)}, u32[]{:S(2)}, u32[]{:S(2)}) %collective-permute-start.4) | collective-permute-done | bytes 266272 | tf_op jit(solution)/shard_map/ppermute | solution.py:47
  242.6 13.2 %collective-permute-done.5 = f32[520,128]{1,0:T(8,128)S(1)} collective-permute-done((f32[520,128]{1,0:T(8,128)S(1)}, f32[520,128]{1,0:T(8,128)S(1)}, u32[]{:S(2)}, u32[]{:S(2)}) %collective-permute-start.5) | collective-permute-done | bytes 266272 | tf_op jit(solution)/shard_map/ppermute | solution.py:47
  256.1 1.8 collective-permute-start.7
  258.0 7.5 %collective-permute-done.7 = f32[520,128]{1,0:T(8,128)S(1)} collective-permute-done((f32[520,128]{1,0:T(8,128)S(1)}, f32[520,128]{1,0:T(8,128)S(1)}, u32[]{:S(2)}, u32[]{:S(2)}) %collective-permute-start.7) | collective-permute-done | bytes 266272 | tf_op jit(solution)/shard_map/ppermute | solution.py:47
  265.5 4.6 %collective-permute-done.8 = f32[520,128]{1,0:T(8,128)S(1)} collective-permute-done((f32[520,128]{1,0:T(8,128)S(1)}, f32[520,128]{1,0:T(8,128)S(1)}, u32[]{:S(2)}, u32[]{:S(2)}) %collective-permute-start.8) | collective-permute-done | bytes 266272 | tf_op jit(solution)/shard_map/ppermute | solution.py:47
  270.5 1.8 fusion.35
  272.3 1.7 fusion.3
  274.0 1.1 fusion.32
  275.1 1.1 fusion.10
  276.7 5.3 %fusion.19 = (f32[128]{0:T(128)S(1)}, f32[128]{0:T(128)S(1)}, f32[128]{0:T(128)S(1)}, f32[1664,128]{1,0:T(8,128)S(1)}) fusion(f32[1664,128]{1,0:T(8,128)S(1)} %get-tuple-element.23, f32[1664]{0:T(1024)S(1)} %get-tuple-element.29, f32[1664]{0:T(1024)S(1)} %get-tuple-element.30, bf16[2048,1664]{1,0:T(8,128)(2,1)} %bitcast.8, ...), kind=kOutput, calls=%fused_computation.41 | convolution fusion | flops 875183744 | bytes 9059328 | tf_op jit(solution)/shard_map/dot_general | solution.py:108
  281.9 6.0 %fusion.24 = f32[2048,128]{1,0:T(8,128)} fusion(bf16[2048,1664]{1,0:T(8,128)(2,1)} %bitcast.8, f32[1664,128]{1,0:T(8,128)S(1)} %get-tuple-element.26, f32[1664]{0:T(1024)S(1)} %get-tuple-element.30), kind=kOutput, calls=%fused_computation.60 | convolution fusion | flops 872841216 | bytes 8722944 | tf_op jit(solution)/shard_map/dot_general | solution.py:113
  287.9 2.3 concatenate.45
  290.3 1.7 collective-permute-start.11
  292.3 6.5 %collective-permute-done.11 = f32[520,128]{1,0:T(8,128)S(1)} collective-permute-done((f32[520,128]{1,0:T(8,128)S(1)}, f32[520,128]{1,0:T(8,128)S(1)}, u32[]{:S(2)}, u32[]{:S(2)}) %collective-permute-start.11) | collective-permute-done | bytes 266272 | tf_op jit(solution)/shard_map/ppermute | solution.py:47
  298.8 5.9 %collective-permute-done.10 = f32[520,128]{1,0:T(8,128)S(1)} collective-permute-done((f32[520,128]{1,0:T(8,128)S(1)}, f32[520,128]{1,0:T(8,128)S(1)}, u32[]{:S(2)}, u32[]{:S(2)}) %collective-permute-start.10) | collective-permute-done | bytes 266272 | tf_op jit(solution)/shard_map/ppermute | solution.py:47
  305.7 7.0 %collective-permute-done.12 = f32[520,128]{1,0:T(8,128)S(1)} collective-permute-done((f32[520,128]{1,0:T(8,128)S(1)}, f32[520,128]{1,0:T(8,128)S(1)}, u32[]{:S(2)}, u32[]{:S(2)}) %collective-permute-start.12) | collective-permute-done | bytes 266272 | tf_op jit(solution)/shard_map/ppermute | solution.py:47
  312.8 7.0 %collective-permute-done.13 = f32[520,128]{1,0:T(8,128)S(1)} collective-permute-done((f32[520,128]{1,0:T(8,128)S(1)}, f32[520,128]{1,0:T(8,128)S(1)}, u32[]{:S(2)}, u32[]{:S(2)}) %collective-permute-start.13) | collective-permute-done | bytes 266272 | tf_op jit(solution)/shard_map/ppermute | solution.py:47
  320.0 12.7 %collective-permute-done.14 = f32[520,128]{1,0:T(8,128)S(1)} collective-permute-done((f32[520,128]{1,0:T(8,128)S(1)}, f32[520,128]{1,0:T(8,128)S(1)}, u32[]{:S(2)}, u32[]{:S(2)}) %collective-permute-start.14) | collective-permute-done | bytes 266272 | tf_op jit(solution)/shard_map/ppermute | solution.py:47
  333.5 1.7 collective-permute-start.16
  336.4 6.6 %collective-permute-done.16 = f32[520,128]{1,0:T(8,128)S(1)} collective-permute-done((f32[520,128]{1,0:T(8,128)}, f32[520,128]{1,0:T(8,128)S(1)}, u32[]{:S(2)}, u32[]{:S(2)}) %collective-permute-start.16) | collective-permute-done | bytes 266272 | tf_op jit(solution)/shard_map/ppermute | solution.py:47
  343.0 4.7 %collective-permute-done.17 = f32[520,128]{1,0:T(8,128)S(1)} collective-permute-done((f32[520,128]{1,0:T(8,128)}, f32[520,128]{1,0:T(8,128)S(1)}, u32[]{:S(2)}, u32[]{:S(2)}) %collective-permute-start.17) | collective-permute-done | bytes 266272 | tf_op jit(solution)/shard_map/ppermute | solution.py:47
  348.1 1.4 multiply_add_fusion
  349.7 1.8 fusion.34
  351.5 1.7 fusion.2
  353.2 1.1 fusion.31
  354.3 1.2 fusion.9
  355.5 4.9 %fusion.44 = f32[1664,128]{1,0:T(8,128)S(1)} fusion(bf16[2048,1664]{1,0:T(8,128)(2,1)} %bitcast.8, bf16[2048,128]{1,0:T(8,128)(2,1)S(1)} %bitcast.212), kind=kOutput, calls=%fused_computation.113 | convolution fusion | flops 872415232 | bytes 8192000 | tf_op jit(solution)/shard_map/dot_general | solution.py:108
  360.8 1.4 dynamic-slice_subtract_fusion
  (85 shorter events, 13.9 us)
Async XLA Ops:
  7.2 9.0 %copy-start = (bf16[256,12544]{1,0:T(8,128)(2,1)S(1)}, bf16[256,12544]{1,0:T(8,128)(2,1)}, u32[]{:S(2)}) copy-start(bf16[256,12544]{1,0:T(8,128)(2,1)} %param.8) | copy-start | bytes 19267588
  20.1 8.2 %copy-start.3 = (s32[256]{0:T(256)S(1)}, s32[256]{0:T(256)}, u32[]{:S(2)}) copy-start(s32[256]{0:T(256)} %param.11) | copy-start | bytes 3076
  20.1 8.2 %copy-start.2 = (f32[256,128]{1,0:T(8,128)S(1)}, f32[256,128]{1,0:T(8,128)}, u32[]{:S(2)}) copy-start(f32[256,128]{1,0:T(8,128)} %param.9) | copy-start | bytes 393220
  20.1 9.1 %copy-start.5 = (s32[8]{0:T(128)S(1)}, s32[8]{0:T(128)}, u32[]{:S(2)}) copy-start(s32[8]{0:T(128)} %constant.80.clone) | copy-start | bytes 100
  20.1 11.6 %copy-start.4 = (f32[128]{0:T(128)S(1)}, f32[128]{0:T(128)}, u32[]{:S(2)}) copy-start(f32[128]{0:T(128)} %param.12) | copy-start | bytes 1540
  20.1 178.9 %all-to-all-start = ((bf16[8,256,1664]{2,1,0:T(8,128)(2,1)}), bf16[8,256,1664]{2,1,0:T(8,128)(2,1)}, u32[]{:S(2)}, u32[]{:S(2)}) async-start(bf16[8,256,1664]{2,1,0:T(8,128)(2,1)} %bitcast_dynamic-update-slice_fusion), calls=%async_computation | async-start | bytes 13631488 | tf_op jit(solution)/shard_map/all_to_all | solution.py:91
  27.5 163.1 %all-gather.3.cloned.1.call-start = ((), (), s32[]{:S(2)}) async-start(), calls=%async_computation.1 | async-start | bytes 1216512 | tf_op jit(solution)/shard_map/all_gather | solution.py:98
  204.3 72.4 %copy-start.1 = (f32[1664,128]{1,0:T(8,128)}, f32[1664,128]{1,0:T(8,128)S(1)}, u32[]{:S(2)}) copy-start(f32[1664,128]{1,0:T(8,128)S(1)} %get-tuple-element.23) | copy-start | bytes 2555908
  210.8 8.9 %collective-permute-start.2 = (f32[520,128]{1,0:T(8,128)}, f32[520,128]{1,0:T(8,128)S(1)}, u32[]{:S(2)}, u32[]{:S(2)}) collective-permute-start(f32[520,128]{1,0:T(8,128)} %get-tuple-element.15), channel_id=1, source_target_pairs={{0,3},{1,2},{2,1},{3,0},{4,7},{5,6},{6,5},{7,4},{8,11},{9,10},{10,... | collective-permute-start | bytes 798728 | tf_op jit(solution)/shard_map/ppermute | solution.py:47
  210.8 14.6 %collective-permute-start.1 = (f32[520,128]{1,0:T(8,128)S(1)}, f32[520,128]{1,0:T(8,128)S(1)}, u32[]{:S(2)}, u32[]{:S(2)}) collective-permute-start(f32[520,128]{1,0:T(8,128)S(1)} %get-tuple-element.16), channel_id=1, source_target_pairs={{0,2},{1,3},{2,0},{3,1},{4,6},{5,7},{6,4},{7,5},{8,10},{9,11},{10,... | collective-permute-start | bytes 798728 | tf_op jit(solution)/shard_map/ppermute | solution.py:47
  212.3 13.1 %collective-permute-start = (f32[520,128]{1,0:T(8,128)S(1)}, f32[520,128]{1,0:T(8,128)}, u32[]{:S(2)}, u32[]{:S(2)}) collective-permute-start(f32[520,128]{1,0:T(8,128)S(1)} %get-tuple-element.14), channel_id=1, source_target_pairs={{0,1},{1,0},{2,3},{3,2},{4,5},{5,4},{6,7},{7,6},{8,9},{9,8},{10,11... | collective-permute-start | bytes 798728 | tf_op jit(solution)/shard_map/ppermute | solution.py:47
  226.5 8.4 %collective-permute-start.3 = (f32[520,128]{1,0:T(8,128)S(1)}, f32[520,128]{1,0:T(8,128)S(1)}, u32[]{:S(2)}, u32[]{:S(2)}) collective-permute-start(f32[520,128]{1,0:T(8,128)S(1)} %fusion.30), channel_id=1, source_target_pairs={{0,4},{4,0},{8,12},{12,8},{16,20},{20,16},{24,28},{28,24},{1,5},{5... | collective-permute-start | bytes 798728 | tf_op jit(solution)/shard_map/ppermute | solution.py:47
  234.9 7.6 %collective-permute-start.4 = (f32[520,128]{1,0:T(8,128)S(1)}, f32[520,128]{1,0:T(8,128)S(1)}, u32[]{:S(2)}, u32[]{:S(2)}) collective-permute-start(f32[520,128]{1,0:T(8,128)S(1)} %add.166), channel_id=1, source_target_pairs={{0,8},{4,12},{8,0},{12,4},{16,24},{20,28},{24,16},{28,20},{1,9},{5... | collective-permute-start | bytes 798728 | tf_op jit(solution)/shard_map/ppermute | solution.py:47
  242.6 13.3 %collective-permute-start.5 = (f32[520,128]{1,0:T(8,128)S(1)}, f32[520,128]{1,0:T(8,128)S(1)}, u32[]{:S(2)}, u32[]{:S(2)}) collective-permute-start(f32[520,128]{1,0:T(8,128)S(1)} %add.167), channel_id=1, source_target_pairs={{0,16},{4,20},{8,24},{12,28},{16,0},{20,4},{24,8},{28,12},{1,17},{... | collective-permute-start | bytes 798728 | tf_op jit(solution)/shard_map/ppermute | solution.py:47
  256.0 1.9 collective-permute-start.6
  256.1 9.3 %collective-permute-start.7 = (f32[520,128]{1,0:T(8,128)S(1)}, f32[520,128]{1,0:T(8,128)S(1)}, u32[]{:S(2)}, u32[]{:S(2)}) collective-permute-start(f32[520,128]{1,0:T(8,128)S(1)} %get-tuple-element.10), channel_id=1, source_target_pairs={{0,2},{1,3},{2,0},{3,1},{4,6},{5,7},{6,4},{7,5},{8,10},{9,11},{10,... | collective-permute-start | bytes 798728 | tf_op jit(solution)/shard_map/ppermute | solution.py:47
  257.9 12.2 %collective-permute-start.8 = (f32[520,128]{1,0:T(8,128)S(1)}, f32[520,128]{1,0:T(8,128)S(1)}, u32[]{:S(2)}, u32[]{:S(2)}) collective-permute-start(f32[520,128]{1,0:T(8,128)S(1)} %get-tuple-element.10), channel_id=1, source_target_pairs={{0,3},{1,2},{2,1},{3,0},{4,7},{5,6},{6,5},{7,4},{8,11},{9,10},{10,... | collective-permute-start | bytes 798728 | tf_op jit(solution)/shard_map/ppermute | solution.py:47
  290.3 8.5 %collective-permute-start.11 = (f32[520,128]{1,0:T(8,128)S(1)}, f32[520,128]{1,0:T(8,128)S(1)}, u32[]{:S(2)}, u32[]{:S(2)}) collective-permute-start(f32[520,128]{1,0:T(8,128)S(1)} %get-tuple-element.12), channel_id=1, source_target_pairs={{0,3},{1,2},{2,1},{3,0},{4,7},{5,6},{6,5},{7,4},{8,11},{9,10},{10,... | collective-permute-start | bytes 798728 | tf_op jit(solution)/shard_map/ppermute | solution.py:47
  292.0 12.7 %collective-permute-start.10 = (f32[520,128]{1,0:T(8,128)S(1)}, f32[520,128]{1,0:T(8,128)S(1)}, u32[]{:S(2)}, u32[]{:S(2)}) collective-permute-start(f32[520,128]{1,0:T(8,128)S(1)} %get-tuple-element.13), channel_id=1, source_target_pairs={{0,2},{1,3},{2,0},{3,1},{4,6},{5,7},{6,4},{7,5},{8,10},{9,11},{10,... | collective-permute-start | bytes 798728 | tf_op jit(solution)/shard_map/ppermute | solution.py:47
  292.3 12.4 %collective-permute-start.9 = (f32[520,128]{1,0:T(8,128)S(1)}, f32[520,128]{1,0:T(8,128)S(1)}, u32[]{:S(2)}, u32[]{:S(2)}) collective-permute-start(f32[520,128]{1,0:T(8,128)S(1)} %get-tuple-element.11), channel_id=1, source_target_pairs={{0,1},{1,0},{2,3},{3,2},{4,5},{5,4},{6,7},{7,6},{8,9},{9,8},{10,11... | collective-permute-start | bytes 798728 | tf_op jit(solution)/shard_map/ppermute | solution.py:47
  304.8 7.9 %collective-permute-start.12 = (f32[520,128]{1,0:T(8,128)S(1)}, f32[520,128]{1,0:T(8,128)S(1)}, u32[]{:S(2)}, u32[]{:S(2)}) collective-permute-start(f32[520,128]{1,0:T(8,128)S(1)} %fusion.28), channel_id=1, source_target_pairs={{0,4},{4,0},{8,12},{12,8},{16,20},{20,16},{24,28},{28,24},{1,5},{5... | collective-permute-start | bytes 798728 | tf_op jit(solution)/shard_map/ppermute | solution.py:47
  312.8 7.1 %collective-permute-start.13 = (f32[520,128]{1,0:T(8,128)S(1)}, f32[520,128]{1,0:T(8,128)S(1)}, u32[]{:S(2)}, u32[]{:S(2)}) collective-permute-start(f32[520,128]{1,0:T(8,128)S(1)} %add.178), channel_id=1, source_target_pairs={{0,8},{4,12},{8,0},{12,4},{16,24},{20,28},{24,16},{28,20},{1,9},{5... | collective-permute-start | bytes 798728 | tf_op jit(solution)/shard_map/ppermute | solution.py:47
  319.9 12.8 %collective-permute-start.14 = (f32[520,128]{1,0:T(8,128)S(1)}, f32[520,128]{1,0:T(8,128)S(1)}, u32[]{:S(2)}, u32[]{:S(2)}) collective-permute-start(f32[520,128]{1,0:T(8,128)S(1)} %add.179), channel_id=1, source_target_pairs={{0,16},{4,20},{8,24},{12,28},{16,0},{20,4},{24,8},{28,12},{1,17},{... | collective-permute-start | bytes 798728 | tf_op jit(solution)/shard_map/ppermute | solution.py:47
  333.5 1.9 collective-permute-start.15
  333.5 9.5 %collective-permute-start.16 = (f32[520,128]{1,0:T(8,128)}, f32[520,128]{1,0:T(8,128)S(1)}, u32[]{:S(2)}, u32[]{:S(2)}) collective-permute-start(f32[520,128]{1,0:T(8,128)} %get-tuple-element.8), channel_id=1, source_target_pairs={{0,2},{1,3},{2,0},{3,1},{4,6},{5,7},{6,4},{7,5},{8,10},{9,11},{10,... | collective-permute-start | bytes 798728 | tf_op jit(solution)/shard_map/ppermute | solution.py:47
  335.3 12.4 %collective-permute-start.17 = (f32[520,128]{1,0:T(8,128)}, f32[520,128]{1,0:T(8,128)S(1)}, u32[]{:S(2)}, u32[]{:S(2)}) collective-permute-start(f32[520,128]{1,0:T(8,128)} %get-tuple-element.8), channel_id=1, source_target_pairs={{0,3},{1,2},{2,1},{3,0},{4,7},{5,6},{6,5},{7,4},{8,11},{9,10},{10,... | collective-permute-start | bytes 798728 | tf_op jit(solution)/shard_map/ppermute | solution.py:47
Sparse Core Ops, SparseCore 0:
  31.1 159.4 all-gather.2

commit v3 on v2

--- a/solution.py
+++ b/solution.py
@@ -94,8 +94,13 @@
     own_weight = ((gap_mask == 1) & (position < slab_counts[0])).astype(jnp.float32)
     columns_count = observed.shape[1]
     weight_rows = own_weight.reshape(-1, columns_count)
-    blank = jnp.zeros((-weight_rows.shape[0] % 8, columns_count), jnp.float32)
-    packed = lax.all_gather(jnp.concatenate([observed, weight_rows, blank]), "tm", axis=0)
+    shares = lax.axis_size("coef")
+    spare = -(epoch_rows + weight_rows.shape[0]) % (8 * shares)
+    packed = jnp.concatenate(
+        [observed, weight_rows, jnp.zeros((spare, columns_count), jnp.float32)]
+    ).reshape(shares, -1, columns_count)
+    share = lax.dynamic_index_in_dim(packed, lax.axis_index("coef"), 0, keepdims=False)
+    packed = lax.all_gather(share, ("tm", "coef"), axis=0).reshape(slabs, -1, columns_count)
     observed_all = packed[:, :epoch_rows].reshape(-1, columns_count)
     weight = packed[:, epoch_rows : epoch_rows + weight_rows.shape[0]].reshape(-1, 1)
     lower_block, upper_block = block_pair(filter_taps)

time: 370 us -> 361 us (0.976)
  waiting for transfers between devices: 261 us -> 248 us
  starting transfers between devices: 16.5 us -> 21.2 us
    all_gather x1, waiting for transfers between devices: 156 us -> 150 us  [shards(): lax.all_gather(share, ('tm', 'coef'), axis=0)]
    ppermute x18, waiting for transfers between devices: 104 us -> 98.4 us  [exchanged(): lax.ppermute(value, axis, [(index, index ^ distance) for index in range(l...]
    ppermute x18, starting transfers between devices: 8.98 us -> 13.7 us  [exchanged(): lax.ppermute(value, axis, [(index, index ^ distance) for index in range(l...]
  transfers between devices with their start and end apart: 20 -> 20, of which waited for: 15 -> 15; matrix products, arithmetic and copies ran while one was open for 3% -> 4% of each run, Pallas kernels for 0% -> 0%
where the time goes in v3:
time: 361 us; the launch traced here: 360 us
  waiting for transfers between devices  248 us (69%)
  matrix products  44.2 us (12%)
  local copies, waits for them, and re-layouts  21.6 us (6%)
  starting transfers between devices  21.2 us (6%)
  between operations  17.7 us (5%)
  other arithmetic  6.76 us (2%)
    all_gather x1, waiting for transfers between devices, shards(): lax.all_gather(share, ('tm', 'coef'), axis=0)  150 us
    ppermute x18, waiting for transfers between devices, exchanged(): lax.ppermute(value, axis, [(index, index ^ distance) for index in range(l...  98.4 us
    dot_general x3, matrix products, transposed(): lax.dot_general(columns, filtered, (((0,), (0,)), ((), ())), preferred_el...  15.4 us
    ppermute x18, starting transfers between devices, exchanged(): lax.ppermute(value, axis, [(index, index ^ distance) for index in range(l...  13.7 us
    unnamed x22, local copies, waits for them, and re-layouts  12.1 us
    dot_general x2, matrix products, reduced(): jnp.dot(columns, vector.astype(jnp.bfloat16), preferred_element_type=jnp....  11.3 us
    all_to_all x1, starting transfers between devices, shards(): lax.all_to_all(pieces, 'tm', 0, 0).reshape(slabs * epoch_rows, window)  7.45 us
  transfers between devices with their start and end apart: 20, of which 15 were waited for; matrix products, arithmetic and copies ran while one was open for 4% of the time, Pallas kernels for 0%

profile of v3, /device:TPU:0, one launch (start us, length us, event | category | flops | bytes accessed | tf_op | source)
XLA Modules:
  0.0 359.8 jit_solution(9343193487401234720)
XLA Ops:
  7.2 2.3 bitcast_dynamic-update-slice_fusion.7
  9.4 2.4 bitcast_dynamic-update-slice_fusion.6
  11.8 2.2 bitcast_dynamic-update-slice_fusion.5
  14.0 2.1 bitcast_dynamic-update-slice_fusion.4
  20.1 7.5 %all-to-all-start = ((bf16[8,256,1664]{2,1,0:T(8,128)(2,1)}), bf16[8,256,1664]{2,1,0:T(8,128)(2,1)}, u32[]{:S(2)}, u32[]{:S(2)}) async-start(bf16[8,256,1664]{2,1,0:T(8,128)(2,1)} %bitcast_dynamic-update-slice_fusion), calls=%async_computation | async-start | bytes 13631488 | tf_op jit(solution)/shard_map/all_to_all | solution.py:91
  34.3 150.0 %all-gather.2.cloned.1.call-done = f32[32,72,128]{2,1,0:T(8,128)} async-done(((f32[1,72,128]{2,1,0:T(8,128)}), f32[32,72,128]{2,1,0:T(8,128)}) %all-gather.2.cloned.1.call-update) | async-done | bytes 1179664 | tf_op jit(solution)/shard_map/all_gather | solution.py:103
  184.3 1.3 slice.129
  186.4 2.1 fusion.11
  188.8 1.7 fusion.4
  190.5 1.1 fusion.33
  191.6 1.1 fusion.6
  192.7 5.2 %fusion.17 = (f32[128]{0:T(128)S(1)}, f32[128]{0:T(128)S(1)}, f32[1664,128]{1,0:T(8,128)S(1)}) fusion(f32[1664]{0:T(1024)S(1)} %get-tuple-element.29, f32[1664]{0:T(1024)S(1)} %get-tuple-element.30, bf16[2048,1664]{1,0:T(8,128)(2,1)} %bitcast.8, bf16[2048,128]{1,0:T(8,128)(2,1)S(1)} %bitcast.225), kind=kOutput, calls=%fused_computation.39 | convolution fusion | flops 873692928 | bytes 8206336 | tf_op jit(solution)/shard_map/dot_general | solution.py:113
  198.0 5.3 %fusion.23 = f32[2048,128]{1,0:T(8,128)S(1)} fusion(bf16[2048,1664]{1,0:T(8,128)(2,1)} %bitcast.8, f32[1664,128]{1,0:T(8,128)S(1)} %get-tuple-element.23, f32[1664]{0:T(1024)S(1)} %get-tuple-element.30), kind=kOutput, calls=%fused_computation.59 | convolution fusion | flops 872841216 | bytes 8722944 | tf_op jit(solution)/shard_map/dot_general | solution.py:118
  203.8 1.4 collective-permute-start.2
  205.7 6.4 %collective-permute-done.2 = f32[520,128]{1,0:T(8,128)S(1)} collective-permute-done((f32[520,128]{1,0:T(8,128)S(1)}, f32[520,128]{1,0:T(8,128)S(1)}, u32[]{:S(2)}, u32[]{:S(2)}) %collective-permute-start.2) | collective-permute-done | bytes 266272 | tf_op jit(solution)/shard_map/ppermute | solution.py:47
  212.2 6.1 %collective-permute-done.1 = f32[520,128]{1,0:T(8,128)S(1)} collective-permute-done((f32[520,128]{1,0:T(8,128)S(1)}, f32[520,128]{1,0:T(8,128)S(1)}, u32[]{:S(2)}, u32[]{:S(2)}) %collective-permute-start.1) | collective-permute-done | bytes 266272 | tf_op jit(solution)/shard_map/ppermute | solution.py:47
  218.4 1.7 collective-permute-start.3
  220.1 6.4 %collective-permute-done.3 = f32[520,128]{1,0:T(8,128)S(1)} collective-permute-done((f32[520,128]{1,0:T(8,128)S(1)}, f32[520,128]{1,0:T(8,128)S(1)}, u32[]{:S(2)}, u32[]{:S(2)}) %collective-permute-start.3) | collective-permute-done | bytes 266272 | tf_op jit(solution)/shard_map/ppermute | solution.py:47
  226.5 7.1 %collective-permute-done.4 = f32[520,128]{1,0:T(8,128)S(1)} collective-permute-done((f32[520,128]{1,0:T(8,128)S(1)}, f32[520,128]{1,0:T(8,128)S(1)}, u32[]{:S(2)}, u32[]{:S(2)}) %collective-permute-start.4) | collective-permute-done | bytes 266272 | tf_op jit(solution)/shard_map/ppermute | solution.py:47
  233.7 1.2 collective-permute-start.5
  234.9 11.7 %collective-permute-done.5 = f32[520,128]{1,0:T(8,128)S(1)} collective-permute-done((f32[520,128]{1,0:T(8,128)S(1)}, f32[520,128]{1,0:T(8,128)S(1)}, u32[]{:S(2)}, u32[]{:S(2)}) %collective-permute-start.5) | collective-permute-done | bytes 266272 | tf_op jit(solution)/shard_map/ppermute | solution.py:47
  246.9 1.6 collective-permute-start.7
  248.8 7.5 %collective-permute-done.7 = f32[520,128]{1,0:T(8,128)S(1)} collective-permute-done((f32[520,128]{1,0:T(8,128)S(1)}, f32[520,128]{1,0:T(8,128)S(1)}, u32[]{:S(2)}, u32[]{:S(2)}) %collective-permute-start.7) | collective-permute-done | bytes 266272 | tf_op jit(solution)/shard_map/ppermute | solution.py:47
  256.3 4.6 %collective-permute-done.8 = f32[520,128]{1,0:T(8,128)S(1)} collective-permute-done((f32[520,128]{1,0:T(8,128)S(1)}, f32[520,128]{1,0:T(8,128)S(1)}, u32[]{:S(2)}, u32[]{:S(2)}) %collective-permute-start.8) | collective-permute-done | bytes 266272 | tf_op jit(solution)/shard_map/ppermute | solution.py:47
  261.3 1.8 fusion.35
  263.1 1.7 fusion.3
  265.9 1.1 fusion.10
  267.4 5.3 %fusion.19 = (f32[128]{0:T(128)S(1)}, f32[128]{0:T(128)S(1)}, f32[128]{0:T(128)S(1)}, f32[1664,128]{1,0:T(8,128)S(1)}) fusion(f32[1664,128]{1,0:T(8,128)S(1)} %get-tuple-element.23, f32[1664]{0:T(1024)S(1)} %get-tuple-element.29, f32[1664]{0:T(1024)S(1)} %get-tuple-element.30, bf16[2048,1664]{1,0:T(8,128)(2,1)} %bitcast.8, ...), kind=kOutput, calls=%fused_computation.41 | convolution fusion | flops 875183744 | bytes 9059328 | tf_op jit(solution)/shard_map/dot_general | solution.py:113
  272.7 6.0 %fusion.24 = f32[2048,128]{1,0:T(8,128)} fusion(bf16[2048,1664]{1,0:T(8,128)(2,1)} %bitcast.8, f32[1664,128]{1,0:T(8,128)S(1)} %get-tuple-element.26, f32[1664]{0:T(1024)S(1)} %get-tuple-element.30), kind=kOutput, calls=%fused_computation.60 | convolution fusion | flops 872841216 | bytes 8722944 | tf_op jit(solution)/shard_map/dot_general | solution.py:118
  278.7 2.3 concatenate.45
  281.0 1.6 collective-permute-start.11
  283.1 6.3 %collective-permute-done.11 = f32[520,128]{1,0:T(8,128)S(1)} collective-permute-done((f32[520,128]{1,0:T(8,128)S(1)}, f32[520,128]{1,0:T(8,128)S(1)}, u32[]{:S(2)}, u32[]{:S(2)}) %collective-permute-start.11) | collective-permute-done | bytes 266272 | tf_op jit(solution)/shard_map/ppermute | solution.py:47
  289.4 6.1 %collective-permute-done.10 = f32[520,128]{1,0:T(8,128)S(1)} collective-permute-done((f32[520,128]{1,0:T(8,128)S(1)}, f32[520,128]{1,0:T(8,128)S(1)}, u32[]{:S(2)}, u32[]{:S(2)}) %collective-permute-start.10) | collective-permute-done | bytes 266272 | tf_op jit(solution)/shard_map/ppermute | solution.py:47
  295.6 1.7 collective-permute-start.12
  297.3 6.2 %collective-permute-done.12 = f32[520,128]{1,0:T(8,128)S(1)} collective-permute-done((f32[520,128]{1,0:T(8,128)S(1)}, f32[520,128]{1,0:T(8,128)S(1)}, u32[]{:S(2)}, u32[]{:S(2)}) %collective-permute-start.12) | collective-permute-done | bytes 266272 | tf_op jit(solution)/shard_map/ppermute | solution.py:47
  303.6 7.0 %collective-permute-done.13 = f32[520,128]{1,0:T(8,128)S(1)} collective-permute-done((f32[520,128]{1,0:T(8,128)S(1)}, f32[520,128]{1,0:T(8,128)S(1)}, u32[]{:S(2)}, u32[]{:S(2)}) %collective-permute-start.13) | collective-permute-done | bytes 266272 | tf_op jit(solution)/shard_map/ppermute | solution.py:47
  310.6 1.2 collective-permute-start.14
  311.9 11.6 %collective-permute-done.14 = f32[520,128]{1,0:T(8,128)S(1)} collective-permute-done((f32[520,128]{1,0:T(8,128)S(1)}, f32[520,128]{1,0:T(8,128)S(1)}, u32[]{:S(2)}, u32[]{:S(2)}) %collective-permute-start.14) | collective-permute-done | bytes 266272 | tf_op jit(solution)/shard_map/ppermute | solution.py:47
  324.3 1.6 collective-permute-start.16
  327.2 6.6 %collective-permute-done.16 = f32[520,128]{1,0:T(8,128)S(1)} collective-permute-done((f32[520,128]{1,0:T(8,128)}, f32[520,128]{1,0:T(8,128)S(1)}, u32[]{:S(2)}, u32[]{:S(2)}) %collective-permute-start.16) | collective-permute-done | bytes 266272 | tf_op jit(solution)/shard_map/ppermute | solution.py:47
  333.8 4.7 %collective-permute-done.17 = f32[520,128]{1,0:T(8,128)S(1)} collective-permute-done((f32[520,128]{1,0:T(8,128)}, f32[520,128]{1,0:T(8,128)S(1)}, u32[]{:S(2)}, u32[]{:S(2)}) %collective-permute-start.17) | collective-permute-done | bytes 266272 | tf_op jit(solution)/shard_map/ppermute | solution.py:47
  338.9 1.4 multiply_add_fusion
  340.4 1.8 fusion.34
  342.3 1.7 fusion.2
  344.0 1.1 fusion.31
  345.1 1.2 fusion.9
  346.2 4.9 %fusion.44 = f32[1664,128]{1,0:T(8,128)S(1)} fusion(bf16[2048,1664]{1,0:T(8,128)(2,1)} %bitcast.8, bf16[2048,128]{1,0:T(8,128)(2,1)S(1)} %bitcast.213), kind=kOutput, calls=%fused_computation.114 | convolution fusion | flops 872415232 | bytes 8192000 | tf_op jit(solution)/shard_map/dot_general | solution.py:113
  351.5 1.4 dynamic-slice_subtract_fusion
  (86 shorter events, 15.9 us)
Async XLA Ops:
  7.2 9.0 %copy-start = (bf16[256,12544]{1,0:T(8,128)(2,1)S(1)}, bf16[256,12544]{1,0:T(8,128)(2,1)}, u32[]{:S(2)}) copy-start(bf16[256,12544]{1,0:T(8,128)(2,1)} %param.8) | copy-start | bytes 19267588
  20.1 8.2 %copy-start.3 = (s32[256]{0:T(256)S(1)}, s32[256]{0:T(256)}, u32[]{:S(2)}) copy-start(s32[256]{0:T(256)} %param.11) | copy-start | bytes 3076
  20.1 8.3 %copy-start.2 = (f32[256,128]{1,0:T(8,128)S(1)}, f32[256,128]{1,0:T(8,128)}, u32[]{:S(2)}) copy-start(f32[256,128]{1,0:T(8,128)} %param.9) | copy-start | bytes 393220
  20.1 9.0 %copy-start.5 = (s32[8]{0:T(128)S(1)}, s32[8]{0:T(128)}, u32[]{:S(2)}) copy-start(s32[8]{0:T(128)} %constant.84.clone) | copy-start | bytes 100
  20.1 11.6 %copy-start.4 = (f32[128]{0:T(128)S(1)}, f32[128]{0:T(128)}, u32[]{:S(2)}) copy-start(f32[128]{0:T(128)} %param.12) | copy-start | bytes 1540
  20.1 172.6 %all-to-all-start = ((bf16[8,256,1664]{2,1,0:T(8,128)(2,1)}), bf16[8,256,1664]{2,1,0:T(8,128)(2,1)}, u32[]{:S(2)}, u32[]{:S(2)}) async-start(bf16[8,256,1664]{2,1,0:T(8,128)(2,1)} %bitcast_dynamic-update-slice_fusion), calls=%async_computation | async-start | bytes 13631488 | tf_op jit(solution)/shard_map/all_to_all | solution.py:91
  27.5 156.7 %all-gather.2.cloned.1.call-start = ((), (), s32[]{:S(2)}) async-start(), calls=%async_computation.1 | async-start | bytes 1216512 | tf_op jit(solution)/shard_map/all_gather | solution.py:103
  198.0 69.5 %copy-start.1 = (f32[1664,128]{1,0:T(8,128)}, f32[1664,128]{1,0:T(8,128)S(1)}, u32[]{:S(2)}) copy-start(f32[1664,128]{1,0:T(8,128)S(1)} %get-tuple-element.23) | copy-start | bytes 2555908
  203.8 8.4 %collective-permute-start.2 = (f32[520,128]{1,0:T(8,128)S(1)}, f32[520,128]{1,0:T(8,128)S(1)}, u32[]{:S(2)}, u32[]{:S(2)}) collective-permute-start(f32[520,128]{1,0:T(8,128)S(1)} %get-tuple-element.15), channel_id=1, source_target_pairs={{0,3},{1,2},{2,1},{3,0},{4,7},{5,6},{6,5},{7,4},{8,11},{9,10},{10,... | collective-permute-start | bytes 798728 | tf_op jit(solution)/shard_map/ppermute | solution.py:47
  205.2 13.1 %collective-permute-start.1 = (f32[520,128]{1,0:T(8,128)S(1)}, f32[520,128]{1,0:T(8,128)S(1)}, u32[]{:S(2)}, u32[]{:S(2)}) collective-permute-start(f32[520,128]{1,0:T(8,128)S(1)} %get-tuple-element.16), channel_id=1, source_target_pairs={{0,2},{1,3},{2,0},{3,1},{4,6},{5,7},{6,4},{7,5},{8,10},{9,11},{10,... | collective-permute-start | bytes 798728 | tf_op jit(solution)/shard_map/ppermute | solution.py:47
  205.7 12.5 %collective-permute-start = (f32[520,128]{1,0:T(8,128)S(1)}, f32[520,128]{1,0:T(8,128)S(1)}, u32[]{:S(2)}, u32[]{:S(2)}) collective-permute-start(f32[520,128]{1,0:T(8,128)S(1)} %get-tuple-element.14), channel_id=1, source_target_pairs={{0,1},{1,0},{2,3},{3,2},{4,5},{5,4},{6,7},{7,6},{8,9},{9,8},{10,11... | collective-permute-start | bytes 798728 | tf_op jit(solution)/shard_map/ppermute | solution.py:47
  218.4 8.1 %collective-permute-start.3 = (f32[520,128]{1,0:T(8,128)S(1)}, f32[520,128]{1,0:T(8,128)S(1)}, u32[]{:S(2)}, u32[]{:S(2)}) collective-permute-start(f32[520,128]{1,0:T(8,128)S(1)} %fusion.30), channel_id=1, source_target_pairs={{0,4},{4,0},{8,12},{12,8},{16,20},{20,16},{24,28},{28,24},{1,5},{5... | collective-permute-start | bytes 798728 | tf_op jit(solution)/shard_map/ppermute | solution.py:47
  226.5 7.2 %collective-permute-start.4 = (f32[520,128]{1,0:T(8,128)S(1)}, f32[520,128]{1,0:T(8,128)S(1)}, u32[]{:S(2)}, u32[]{:S(2)}) collective-permute-start(f32[520,128]{1,0:T(8,128)S(1)} %add.168), channel_id=1, source_target_pairs={{0,8},{4,12},{8,0},{12,4},{16,24},{20,28},{24,16},{28,20},{1,9},{5... | collective-permute-start | bytes 798728 | tf_op jit(solution)/shard_map/ppermute | solution.py:47
  233.7 13.0 %collective-permute-start.5 = (f32[520,128]{1,0:T(8,128)S(1)}, f32[520,128]{1,0:T(8,128)S(1)}, u32[]{:S(2)}, u32[]{:S(2)}) collective-permute-start(f32[520,128]{1,0:T(8,128)S(1)} %add.169), channel_id=1, source_target_pairs={{0,16},{4,20},{8,24},{12,28},{16,0},{20,4},{24,8},{28,12},{1,17},{... | collective-permute-start | bytes 798728 | tf_op jit(solution)/shard_map/ppermute | solution.py:47
  246.8 1.9 collective-permute-start.6
  246.9 9.3 %collective-permute-start.7 = (f32[520,128]{1,0:T(8,128)S(1)}, f32[520,128]{1,0:T(8,128)S(1)}, u32[]{:S(2)}, u32[]{:S(2)}) collective-permute-start(f32[520,128]{1,0:T(8,128)S(1)} %get-tuple-element.10), channel_id=1, source_target_pairs={{0,2},{1,3},{2,0},{3,1},{4,6},{5,7},{6,4},{7,5},{8,10},{9,11},{10,... | collective-permute-start | bytes 798728 | tf_op jit(solution)/shard_map/ppermute | solution.py:47
  248.5 12.4 %collective-permute-start.8 = (f32[520,128]{1,0:T(8,128)S(1)}, f32[520,128]{1,0:T(8,128)S(1)}, u32[]{:S(2)}, u32[]{:S(2)}) collective-permute-start(f32[520,128]{1,0:T(8,128)S(1)} %get-tuple-element.10), channel_id=1, source_target_pairs={{0,3},{1,2},{2,1},{3,0},{4,7},{5,6},{6,5},{7,4},{8,11},{9,10},{10,... | collective-permute-start | bytes 798728 | tf_op jit(solution)/shard_map/ppermute | solution.py:47
  281.0 8.4 %collective-permute-start.11 = (f32[520,128]{1,0:T(8,128)S(1)}, f32[520,128]{1,0:T(8,128)S(1)}, u32[]{:S(2)}, u32[]{:S(2)}) collective-permute-start(f32[520,128]{1,0:T(8,128)S(1)} %get-tuple-element.12), channel_id=1, source_target_pairs={{0,3},{1,2},{2,1},{3,0},{4,7},{5,6},{6,5},{7,4},{8,11},{9,10},{10,... | collective-permute-start | bytes 798728 | tf_op jit(solution)/shard_map/ppermute | solution.py:47
  282.6 12.9 %collective-permute-start.10 = (f32[520,128]{1,0:T(8,128)S(1)}, f32[520,128]{1,0:T(8,128)S(1)}, u32[]{:S(2)}, u32[]{:S(2)}) collective-permute-start(f32[520,128]{1,0:T(8,128)S(1)} %get-tuple-element.13), channel_id=1, source_target_pairs={{0,2},{1,3},{2,0},{3,1},{4,6},{5,7},{6,4},{7,5},{8,10},{9,11},{10,... | collective-permute-start | bytes 798728 | tf_op jit(solution)/shard_map/ppermute | solution.py:47
  283.1 12.4 %collective-permute-start.9 = (f32[520,128]{1,0:T(8,128)S(1)}, f32[520,128]{1,0:T(8,128)S(1)}, u32[]{:S(2)}, u32[]{:S(2)}) collective-permute-start(f32[520,128]{1,0:T(8,128)S(1)} %get-tuple-element.11), channel_id=1, source_target_pairs={{0,1},{1,0},{2,3},{3,2},{4,5},{5,4},{6,7},{7,6},{8,9},{9,8},{10,11... | collective-permute-start | bytes 798728 | tf_op jit(solution)/shard_map/ppermute | solution.py:47
  295.6 7.9 %collective-permute-start.12 = (f32[520,128]{1,0:T(8,128)S(1)}, f32[520,128]{1,0:T(8,128)S(1)}, u32[]{:S(2)}, u32[]{:S(2)}) collective-permute-start(f32[520,128]{1,0:T(8,128)S(1)} %fusion.28), channel_id=1, source_target_pairs={{0,4},{4,0},{8,12},{12,8},{16,20},{20,16},{24,28},{28,24},{1,5},{5... | collective-permute-start | bytes 798728 | tf_op jit(solution)/shard_map/ppermute | solution.py:47
  303.5 7.1 %collective-permute-start.13 = (f32[520,128]{1,0:T(8,128)S(1)}, f32[520,128]{1,0:T(8,128)S(1)}, u32[]{:S(2)}, u32[]{:S(2)}) collective-permute-start(f32[520,128]{1,0:T(8,128)S(1)} %add.180), channel_id=1, source_target_pairs={{0,8},{4,12},{8,0},{12,4},{16,24},{20,28},{24,16},{28,20},{1,9},{5... | collective-permute-start | bytes 798728 | tf_op jit(solution)/shard_map/ppermute | solution.py:47
  310.6 12.8 %collective-permute-start.14 = (f32[520,128]{1,0:T(8,128)S(1)}, f32[520,128]{1,0:T(8,128)S(1)}, u32[]{:S(2)}, u32[]{:S(2)}) collective-permute-start(f32[520,128]{1,0:T(8,128)S(1)} %add.181), channel_id=1, source_target_pairs={{0,16},{4,20},{8,24},{12,28},{16,0},{20,4},{24,8},{28,12},{1,17},{... | collective-permute-start | bytes 798728 | tf_op jit(solution)/shard_map/ppermute | solution.py:47
  324.3 1.9 collective-permute-start.15
  324.3 9.5 %collective-permute-start.16 = (f32[520,128]{1,0:T(8,128)}, f32[520,128]{1,0:T(8,128)S(1)}, u32[]{:S(2)}, u32[]{:S(2)}) collective-permute-start(f32[520,128]{1,0:T(8,128)} %get-tuple-element.8), channel_id=1, source_target_pairs={{0,2},{1,3},{2,0},{3,1},{4,6},{5,7},{6,4},{7,5},{8,10},{9,11},{10,... | collective-permute-start | bytes 798728 | tf_op jit(solution)/shard_map/ppermute | solution.py:47
  325.9 12.6 %collective-permute-start.17 = (f32[520,128]{1,0:T(8,128)}, f32[520,128]{1,0:T(8,128)S(1)}, u32[]{:S(2)}, u32[]{:S(2)}) collective-permute-start(f32[520,128]{1,0:T(8,128)} %get-tuple-element.8), channel_id=1, source_target_pairs={{0,3},{1,2},{2,1},{3,0},{4,7},{5,6},{6,5},{7,4},{8,11},{9,10},{10,... | collective-permute-start | bytes 798728 | tf_op jit(solution)/shard_map/ppermute | solution.py:47
Sparse Core Ops, SparseCore 0:
  31.8 152.4 all-gather.1
